TPU v7x, 32 devices: a whole 2x2x4 slice. The times are simulated.
32 devices in a mesh: samp: 16 (over z, y, core), feat: 2 (over x).
Axes of the slice: x: 2, y: 2, z: 4, core: 2. Of those that a mesh axis runs over, the one named last changes fastest.
Arguments:
- grads: bfloat16 [8192, 4096], P('samp', 'feat'), may hold values from -60 to 60
- weights: float32 [8192], P('samp'), may hold values from 0.05 to 6
- targets: float32 [4096, 64], P('feat'), may hold values from -6 to 6
Outputs:
- scores: float32 [8192, 64], P(('samp', 'feat'))
- solution: float32 [4096, 64], P('feat')
- residual: float32 [4096, 64], P('feat')
All inputs are finite; a program needn't handle non-finite values.
Results may differ from a plain program's by a relative error of at most 0.014.
Values may be sent and summed in bfloat16 or wider, within the bound.
A program may use at most 64 MiB of HBM per device.

v0:
```python
import math

import jax
import jax.numpy as jnp
from jax import lax
from jax.sharding import PartitionSpec as P

ITERS = 2


damping_term = 0.1


def per_device(grads, weights, targets):
    rows_dev, feat_cols = grads.shape
    n_samp = lax.axis_size("samp")
    n_feat = lax.axis_size("feat")
    total = rows_dev * n_samp
    full_width = feat_cols * n_feat
    share = rows_dev // n_feat
    offset = lax.axis_index("feat") * share
    scaled = weights / total
    regrouped = lax.all_to_all(grads, "feat", split_axis=0, concat_axis=1, tiled=True)
    own_weights = lax.dynamic_slice_in_dim(scaled, offset, share, 0)

    def column_norms(resid):
        squares = jnp.sum(resid * resid, axis=0)
        parts = (squares,)
        return lax.psum((parts[0],), "feat")

    solution = jnp.zeros_like(targets)
    resid = targets
    direction = targets
    accum = jnp.zeros((share, targets.shape[1]), jnp.float32)
    norm_now = column_norms(resid)[0]
    for step in range(ITERS):
        packed = direction.astype(jnp.bfloat16)
        sample_rows = jnp.dot(
            regrouped,
            lax.all_gather(packed, "feat", axis=0, tiled=True),
            preferred_element_type=jnp.float32,
        )
        weighted = (sample_rows * own_weights[:, None]).astype(jnp.bfloat16)
        partial_image = lax.psum_scatter(
            lax.dot_general(
                regrouped, weighted, (((0,), (0,)), ((), ())), preferred_element_type=jnp.float32
            ).astype(jnp.bfloat16),
            "feat",
            scatter_dimension=0,
            tiled=True,
        ).astype(jnp.float32)
        own_rows = sample_rows
        apply_own_weights = own_weights
        image = lax.psum(partial_image, "samp") + damping_term * direction
        own_rows, own_weights, image = (own_rows, apply_own_weights, image)
        curvature = lax.psum(jnp.sum(direction * image, axis=0), "feat")
        alpha = norm_now / curvature
        solution = solution + alpha * direction
        resid = resid - alpha * image
        accum = accum + alpha * own_rows
        if step + 1 < ITERS:
            sums = column_norms(resid)
            norm_next = sums[0]
            ratio = norm_next / norm_now
            direction = resid + ratio * direction
            norm_now = norm_next
    scores = accum / math.sqrt(full_width)
    return (scores, solution, resid)


def solution(mesh):
    return jax.shard_map(
        per_device,
        mesh=mesh,
        in_specs=(P("samp", "feat"), P("samp"), P("feat", None)),
        out_specs=(P(("samp", "feat"), None), P("feat", None), P("feat", None)),
        check_vma=False,
    )
```

profile of v0, /device:TPU:0, one launch (start us, length us, event | category | flops | bytes accessed | tf_op | source)
XLA Modules:
  0.0 243.3 jit_solution(15761200266702989709)
XLA Ops:
  7.2 0.0 copy-start
  7.2 0.0 copy-start.3
  7.2 4.4 %all-to-all-start = ((bf16[2,256,2048]{2,1,0:T(8,128)(2,1)}), bf16[2,256,2048]{2,1,0:T(8,128)(2,1)S(1)}, u32[]{:S(2)}, u32[]{:S(2)}) async-start(bf16[2,256,2048]{2,1,0:T(8,128)(2,1)} %bitcast.22), calls=%async_computation | async-start | bytes 4194304 | tf_op jit(solution)/shard_map/all_to_all | solution.py:23
  11.6 0.0 reduce-scatter.3.cloned.1.call-start
  11.6 0.0 copy-done
  11.6 0.0 copy-done.3
  11.6 0.1 dynamic_slice.3
  11.7 31.4 %all_gather.6 = bf16[4096,64]{0,1:T(8,128)(2,1)} all-gather(bf16[2048,64]{0,1:T(8,128)(2,1)S(1)} %convert_element_type.31), channel_id=1, replica_groups=mesh['samp'=16,'feat'=2] {'feat'}, dimensions={0}, use_global_device_ids=true | all-gather | bytes 786432 | tf_op jit(solution)/shard_map/all_gather | solution.py:40
  43.1 0.0 all-to-all-done
  43.1 0.0 copy-start.1
  43.1 1.4 copy-done.1
  44.5 0.0 copy-start.2
  44.5 2.9 %copy.6 = bf16[256,2,2048]{0,2,1:T(8,128)(2,1)S(1)} copy(bf16[256,2,2048]{2,0,1:T(8,128)(2,1)} %bitcast.21) | data formatting | bytes 4194304 | tf_op jit(solution)/shard_map/all_to_all | solution.py:23
  47.4 0.0 copy-done.2
  47.4 0.5 fusion.7
  47.9 1.6 fusion
  49.4 0.0 reduce-scatter.3.cloned.1.call-update
  49.5 0.0 reduce-scatter.5.cloned.1.call-start
  49.5 15.3 %reduce-scatter.3.cloned.1.call-done = bf16[2048,64]{0,1:T(8,128)(2,1)} async-done(((bf16[4096,64]{0,1:T(8,128)(2,1)}), bf16[2048,64]{0,1:T(8,128)(2,1)}) %reduce-scatter.3.cloned.1.call-update) | async-done | bytes 262160 | tf_op jit(solution)/shard_map/reduce_scatter | solution.py:44
  64.8 66.8 %all-reduce.3 = f32[2048,64]{0,1:T(8,128)S(1)} all-reduce(bf16[2048,64]{0,1:T(8,128)(2,1)} %reduce-scatter.3.cloned.1.call-done), channel_id=1, replica_groups=mesh['samp'=16,'feat'=2] {'samp'}, use_global_device_ids=true, to_apply=%region_3.0 | all-reduce | flops 131072 | bytes 786432 | tf_op jit(solution)/shard_map/psum | solution.py:54
  131.6 0.2 multiply_reduce_fusion.2
  131.8 4.9 %all-reduce = (f32[64]{0:T(128)S(1)}, f32[64]{0:T(128)S(1)}) all-reduce(f32[64]{0:T(128)S(1)} %get-tuple-element.4, f32[64]{0:T(128)S(1)} %get-tuple-element.3), channel_id=1, replica_groups=mesh['samp'=16,'feat'=2] {'feat'}, use_global_device_ids=true, to_apply=%region_1.0 | all-reduce | flops 128 | bytes 1024 | tf_op jit(solution)/shard_map/psum | solution.py:29
  136.8 0.3 multiply_reduce_fusion.1
  137.0 4.9 %psum.45 = f32[64]{0:T(128)S(1)} all-reduce(f32[64]{0:T(128)S(1)} %multiply_reduce_fusion.1), channel_id=1, replica_groups=mesh['samp'=16,'feat'=2] {'feat'}, use_global_device_ids=true, to_apply=%region_7.0 | all-reduce | flops 64 | bytes 512 | tf_op jit(solution)/shard_map/psum | solution.py:29
  142.0 0.2 fusion.5
  142.2 7.0 %all_gather.7 = bf16[4096,64]{0,1:T(8,128)(2,1)S(1)} all-gather(bf16[2048,64]{0,1:T(8,128)(2,1)S(1)} %fusion.5), channel_id=1, replica_groups=mesh['samp'=16,'feat'=2] {'feat'}, dimensions={0}, use_global_device_ids=true | all-gather | bytes 786432 | tf_op jit(solution)/shard_map/all_gather | solution.py:40
  149.2 0.5 fusion.6
  149.7 1.5 fusion.1
  151.2 0.0 reduce-scatter.5.cloned.1.call-update
  151.2 11.1 %reduce-scatter.5.cloned.1.call-done = bf16[2048,64]{0,1:T(8,128)(2,1)} async-done(((bf16[4096,64]{0,1:T(8,128)(2,1)}), bf16[2048,64]{0,1:T(8,128)(2,1)}) %reduce-scatter.5.cloned.1.call-update) | async-done | bytes 262160 | tf_op jit(solution)/shard_map/reduce_scatter | solution.py:44
  162.4 66.8 %all-reduce.4 = f32[2048,64]{0,1:T(8,128)S(1)} all-reduce(bf16[2048,64]{0,1:T(8,128)(2,1)} %reduce-scatter.5.cloned.1.call-done), channel_id=1, replica_groups=mesh['samp'=16,'feat'=2] {'samp'}, use_global_device_ids=true, to_apply=%region_9.0 | all-reduce | flops 131072 | bytes 786432 | tf_op jit(solution)/shard_map/psum | solution.py:54
  229.2 0.3 multiply_reduce_fusion
  229.5 4.9 %psum.47 = f32[64]{0:T(128)S(1)} all-reduce(f32[64]{0:T(128)S(1)} %multiply_reduce_fusion), channel_id=1, replica_groups=mesh['samp'=16,'feat'=2] {'feat'}, use_global_device_ids=true, to_apply=%region_11.0 | all-reduce | flops 64 | bytes 512 | tf_op jit(solution)/shard_map/psum | solution.py:56
  234.4 0.7 fusion.2
  235.2 1.3 multiply_subtract_fusion
  (5 shorter events, 0.1 us)
Async XLA Ops:
  7.2 4.4 %copy-start = (f32[2048,64]{0,1:T(8,128)S(1)}, f32[2048,64]{0,1:T(8,128)}, u32[]{:S(2)}) copy-start(f32[2048,64]{0,1:T(8,128)} %param.5) | copy-start | bytes 1572868
  7.2 4.4 %copy-start.3 = (f32[512]{0:T(512)S(1)}, f32[512]{0:T(512)}, u32[]{:S(2)}) copy-start(f32[512]{0:T(512)} %param.4) | copy-start | bytes 6148
  7.2 36.0 %all-to-all-start = ((bf16[2,256,2048]{2,1,0:T(8,128)(2,1)}), bf16[2,256,2048]{2,1,0:T(8,128)(2,1)S(1)}, u32[]{:S(2)}, u32[]{:S(2)}) async-start(bf16[2,256,2048]{2,1,0:T(8,128)(2,1)} %bitcast.22), calls=%async_computation | async-start | bytes 4194304 | tf_op jit(solution)/shard_map/all_to_all | solution.py:23
  11.6 53.3 %reduce-scatter.3.cloned.1.call-start = ((), (), s32[]{:S(2)}) async-start(), calls=%async_computation.3 | async-start | bytes 786432 | tf_op jit(solution)/shard_map/reduce_scatter | solution.py:44
  43.1 1.4 copy-start.1
  44.5 2.9 %copy-start.2 = (bf16[4096,64]{0,1:T(8,128)(2,1)S(1)}, bf16[4096,64]{0,1:T(8,128)(2,1)}, u32[]{:S(2)}) copy-start(bf16[4096,64]{0,1:T(8,128)(2,1)} %all_gather.6) | copy-start | bytes 1572868
  49.5 112.9 %reduce-scatter.5.cloned.1.call-start = ((), (), s32[]{:S(2)}) async-start(), calls=%async_computation.4 | async-start | bytes 786432 | tf_op jit(solution)/shard_map/reduce_scatter | solution.py:44
Sparse Core Ops, SparseCore 0:
  49.6 15.1 reduce-scatter.2
  151.4 10.9 reduce-scatter.4
where the time goes:
time: 244 us; the launch traced here: 243 us
  blocking collectives  187 us (77%)
  waiting for transfers between devices  26.5 us (11%)
  between operations  14.1 us (6%)
  starting transfers between devices  4.42 us (2%)
  local copies, waits for them, and re-layouts  4.35 us (2%)
  matrix products  4.03 us (2%)
  other arithmetic  3.03 us (1%)
    psum x2, blocking collectives, per_device(): image = lax.psum(partial_image, 'samp') + damping_term * direction  134 us
    all_gather x2, blocking collectives, per_device(): lax.all_gather(packed, 'feat', axis=0, tiled=True)  38.5 us
    reduce_scatter x2, waiting for transfers between devices, per_device(): lax.psum_scatter(lax.dot_general(regrouped, weighted, (((0,), (0,)), ((),...  26.4 us
    psum x2, blocking collectives, column_norms(): return lax.psum((parts[0],), 'feat')  9.85 us
    psum x1, blocking collectives, per_device(): curvature = lax.psum(jnp.sum(direction * image, axis=0), 'feat')  4.93 us
  transfers between devices with their start and end apart: 3, of which 2 were waited for; matrix products, arithmetic and copies ran while one was open for 0% of the time, Pallas kernels for 0%

commit v1 on v0

--- a/solution.py
+++ b/solution.py
@@ -1,14 +1,240 @@
+import functools
 import math
 
 import jax
 import jax.numpy as jnp
 from jax import lax
+from jax.experimental import pallas as pl
+from jax.experimental.pallas import tpu as pltpu
 from jax.sharding import PartitionSpec as P
 
 ITERS = 2
-
+LANES = 128
+MESH = pl.DeviceIdType.MESH
 
 damping_term = 0.1
+
+
+def pack_columns(columns):
+    dirs = columns[0].shape[0]
+    lane = lax.broadcasted_iota(jnp.int32, (dirs, LANES), 1)
+    tile = jnp.zeros((dirs, LANES), jnp.float32)
+    for position, column in enumerate(columns):
+        tile = jnp.where(lane == position, column, tile)
+    if dirs < LANES:
+        tile = jnp.concatenate([tile, jnp.zeros((LANES - dirs, LANES), jnp.float32)], axis=0)
+    return tile.T[:8]
+
+
+def unpack_columns(tile, count, dirs):
+    padded = jnp.concatenate([tile, jnp.zeros((LANES - 8, LANES), jnp.float32)], axis=0).T
+    return [padded[:dirs, i : i + 1] for i in range(count)]
+
+
+def kernel(
+    chips, total, full_width,
+    grads_ref, weights_ref, targets_ref,
+    scores_ref, solution_ref, resid_ref,
+    rows_out, rows_in, tile_out, tile_in,
+    image_f32, image_b16, pair_in, pair_tile_out, pair_tile_in,
+    chip_out, chip_in, chip_tiles, gathered,
+    feat_send, feat_recv, pair_send, pair_recv, chip_send, chip_recv,
+):
+    samp, feat = lax.axis_index("samp"), lax.axis_index("feat")
+    core = lax.rem(samp, 2)
+    chip = lax.div(samp, 2)
+    dirs, width = targets_ref.shape
+    rows_dev = grads_ref.shape[0]
+    partner = (samp + 1 - 2 * core, feat)
+    mirror = (samp, 1 - feat)
+
+    def peer(offset):
+        other = lax.rem(chip + offset, chips)
+        return other, (other * 2 + core, feat)
+
+    barrier = pltpu.get_barrier_semaphore()
+    for device in [partner, mirror] + [peer(d)[1] for d in range(1, chips)]:
+        pl.semaphore_signal(barrier, inc=1, device_id=device, device_id_type=MESH)
+
+    def remote(src, dst, send, recv, device):
+        return pltpu.make_async_remote_copy(
+            src_ref=src, dst_ref=dst, send_sem=send, recv_sem=recv, device_id=device, device_id_type=MESH
+        )
+
+    scaled = weights_ref[...] / total
+    own_lanes = pl.ds(pl.multiple_of((core * chips + chip) * LANES, LANES), LANES)
+    target_slice = targets_ref[:, own_lanes]
+
+    for step in range(ITERS):
+        targets = targets_ref[...]
+        if step == 0:
+            packed = targets.astype(jnp.bfloat16)
+            sums = [jnp.sum(targets * targets, axis=1, keepdims=True)]
+        else:
+            packed = jnp.concatenate(
+                [gathered[step - 1, c, i] for c in range(2) for i in range(chips)], axis=1
+            )
+            wide = packed.astype(jnp.float32)
+            sums = [
+                jnp.sum(wide * wide, axis=1, keepdims=True),
+                jnp.sum(wide * targets, axis=1, keepdims=True),
+            ]
+        own = lax.dot_general(
+            packed, grads_ref[...], (((1,), (1,)), ((), ())), preferred_element_type=jnp.float32
+        )
+        rows_out[step] = own.astype(jnp.bfloat16)
+        tile_out[step] = pack_columns(sums)
+        if step == 0:
+            pl.semaphore_wait(barrier, chips + 1)
+        copies = [
+            remote(rows_out.at[step], rows_in.at[step], feat_send.at[step, 0], feat_recv.at[step, 0], mirror),
+            remote(tile_out.at[step], tile_in.at[step], feat_send.at[step, 1], feat_recv.at[step, 1], mirror),
+        ]
+        for copy in copies:
+            copy.start()
+        for copy in copies:
+            copy.wait()
+        rows = own + rows_in[step].astype(jnp.float32)
+        sums = unpack_columns(tile_out[step] + tile_in[step], len(sums), dirs)
+        if step == 0:
+            norm = square = sums[0]
+            resid_slice = target_slice
+            direction_slice = target_slice
+            first_rows = rows
+            first_norm = norm
+        else:
+            norm = sums[0]
+            ratio = norm / first_norm
+            square = norm + 2.0 * ratio * sums[1] + ratio * ratio * first_norm
+            rows = rows + ratio * first_rows
+            direction_slice = resid_slice + ratio * target_slice
+        weighted = (rows * scaled).astype(jnp.bfloat16)
+        curve = jnp.sum(weighted.astype(jnp.float32) * rows, axis=1, keepdims=True)
+        image = jnp.dot(weighted, grads_ref[...], preferred_element_type=jnp.float32)
+        for c in range(2):
+            for i in range(chips):
+                at = (c * chips + i) * LANES
+                block = image[:, at : at + LANES]
+                image_f32[c, i] = block
+                image_b16[step, c, i] = block.astype(jnp.bfloat16)
+        pair_tile_out[step] = pack_columns([curve])
+        copies = [
+            remote(image_b16.at[step, 1 - core], pair_in.at[step], pair_send.at[step, 0], pair_recv.at[step, 0], partner),
+            remote(pair_tile_out.at[step], pair_tile_in.at[step], pair_send.at[step, 1], pair_recv.at[step, 1], partner),
+        ]
+        for copy in copies:
+            copy.start()
+        for copy in copies:
+            copy.wait()
+        image_f32[core] = image_f32[core] + pair_in[step].astype(jnp.float32)
+        chip_out[step] = image_f32[core].astype(jnp.bfloat16)
+        chip_tiles[step, chip] = pair_tile_out[step] + pair_tile_in[step]
+        sends = []
+        for d in range(1, chips):
+            other, device = peer(d)
+            sends.append(remote(
+                chip_out.at[step, other], chip_in.at[step, chip],
+                chip_send.at[step, 0, d], chip_recv.at[step, 0, chip], device))
+            sends.append(remote(
+                chip_tiles.at[step, chip], chip_tiles.at[step, chip],
+                chip_send.at[step, 1, d], chip_recv.at[step, 1, chip], device))
+        for copy in sends:
+            copy.start()
+        reduced = image_f32[core, chip]
+        for d in range(1, chips):
+            other, device = peer(d)
+            remote(
+                chip_out.at[step, other], chip_in.at[step, other],
+                chip_send.at[step, 0, d], chip_recv.at[step, 0, other], device).wait_recv()
+            reduced = reduced + chip_in[step, other].astype(jnp.float32)
+            remote(
+                chip_tiles.at[step, other], chip_tiles.at[step, other],
+                chip_send.at[step, 1, d], chip_recv.at[step, 1, other], device).wait_recv()
+        curve_tile = chip_tiles[step, 0]
+        for i in range(1, chips):
+            curve_tile = curve_tile + chip_tiles[step, i]
+        curvature = unpack_columns(curve_tile, 1, dirs)[0] + damping_term * square
+        alpha = norm / curvature
+        resid_slice = resid_slice - alpha * (reduced + damping_term * direction_slice)
+        gathered[step, core, chip] = resid_slice.astype(jnp.bfloat16)
+        spread = []
+        for d in range(1, chips):
+            other, device = peer(d)
+            spread.append(remote(
+                gathered.at[step, core, chip], gathered.at[step, core, chip],
+                chip_send.at[step, 2, d], chip_recv.at[step, 2, chip], device))
+        for copy in spread:
+            copy.start()
+        if step == 0:
+            first_alpha = alpha
+        else:
+            scores = (first_alpha * first_rows + alpha * rows) / math.sqrt(full_width)
+            share = rows_dev // 2
+            scores_ref[...] = jnp.where(feat == 0, scores[:, :share], scores[:, share:])
+            solution_ref[...] = first_alpha * targets + alpha * (wide + ratio * targets)
+        for copy in sends:
+            copy.wait_send()
+        for d in range(1, chips):
+            other, device = peer(d)
+            remote(
+                gathered.at[step, core, other], gathered.at[step, core, other],
+                chip_send.at[step, 2, d], chip_recv.at[step, 2, other], device).wait_recv()
+        swap = remote(
+            gathered.at[step, core], gathered.at[step, core],
+            pair_send.at[step, 2], pair_recv.at[step, 2], partner)
+        swap.start()
+        for copy in spread:
+            copy.wait_send()
+        swap.wait_send()
+        remote(
+            gathered.at[step, 1 - core], gathered.at[step, 1 - core],
+            pair_send.at[step, 2], pair_recv.at[step, 2], partner).wait_recv()
+    for c in range(2):
+        for i in range(chips):
+            at = (c * chips + i) * LANES
+            resid_ref[:, at : at + LANES] = gathered[ITERS - 1, c, i].astype(jnp.float32)
+
+
+def fused(grads, weights, targets):
+    rows_dev, feat_cols = grads.shape
+    n_samp = lax.axis_size("samp")
+    n_feat = lax.axis_size("feat")
+    dirs = targets.shape[1]
+    chips = n_samp // 2
+    f32, b16 = jnp.float32, jnp.bfloat16
+    vmem = pl.BlockSpec(memory_space=pltpu.VMEM)
+    dma = pltpu.SemaphoreType.DMA
+    scores, solved, resid = pl.pallas_call(
+        functools.partial(kernel, chips, rows_dev * n_samp, feat_cols * n_feat),
+        out_shape=(
+            jax.ShapeDtypeStruct((dirs, rows_dev // n_feat), f32),
+            jax.ShapeDtypeStruct((dirs, feat_cols), f32),
+            jax.ShapeDtypeStruct((dirs, feat_cols), f32),
+        ),
+        in_specs=[vmem] * 3,
+        out_specs=[vmem] * 3,
+        scratch_shapes=[
+            pltpu.VMEM((ITERS, dirs, rows_dev), b16),
+            pltpu.VMEM((ITERS, dirs, rows_dev), b16),
+            pltpu.VMEM((ITERS, 8, LANES), f32),
+            pltpu.VMEM((ITERS, 8, LANES), f32),
+            pltpu.VMEM((2, chips, dirs, LANES), f32),
+            pltpu.VMEM((ITERS, 2, chips, dirs, LANES), b16),
+            pltpu.VMEM((ITERS, chips, dirs, LANES), b16),
+            pltpu.VMEM((ITERS, 8, LANES), f32),
+            pltpu.VMEM((ITERS, 8, LANES), f32),
+            pltpu.VMEM((ITERS, chips, dirs, LANES), b16),
+            pltpu.VMEM((ITERS, chips, dirs, LANES), b16),
+            pltpu.VMEM((ITERS, chips, 8, LANES), f32),
+            pltpu.VMEM((ITERS, 2, chips, dirs, LANES), b16),
+            dma((ITERS, 2)), dma((ITERS, 2)),
+            dma((ITERS, 3)), dma((ITERS, 3)),
+            dma((ITERS, 3, chips)), dma((ITERS, 3, chips)),
+        ],
+        compiler_params=pltpu.CompilerParams(collective_id=0, has_side_effects=True),
+        name="cg",
+    )(grads, weights[None, :], targets.T)
+    return scores.T, solved.T, resid.T
 
 
 def per_device(grads, weights, targets):
@@ -68,9 +294,24 @@
     return (scores, solution, resid)
 
 
+def dispatch(grads, weights, targets):
+    rows_dev, feat_cols = grads.shape
+    n_samp, n_feat = lax.axis_size("samp"), lax.axis_size("feat")
+    fits = (
+        n_feat == 2
+        and n_samp % 2 == 0
+        and n_samp >= 4
+        and feat_cols == n_samp * LANES
+        and rows_dev % (2 * LANES) == 0
+        and targets.shape[1] % 16 == 0
+        and targets.shape[1] <= LANES
+    )
+    return (fused if fits else per_device)(grads, weights, targets)
+
+
 def solution(mesh):
     return jax.shard_map(
-        per_device,
+        dispatch,
         mesh=mesh,
         in_specs=(P("samp", "feat"), P("samp"), P("feat", None)),
         out_specs=(P(("samp", "feat"), None), P("feat", None), P("feat", None)),

time: 244 us -> 50.2 us (0.21)
  blocking collectives: 187 us -> 0 us
  Pallas kernels: 0 us -> 44 us
  waiting for transfers between devices: 26.5 us -> 0 us
  between operations: 14.1 us -> 0.64 us
  starting transfers between devices: 4.42 us -> 0 us
  matrix products: 4.03 us -> 0 us
  other arithmetic: 3.03 us -> 0 us
    psum x5 -> x0, blocking collectives: 148 us -> none  [the longest x2 134 us: per_device(): image = lax.psum(partial_image, 'samp') + damping_term * direction]
    pallas_call x0 -> x1, Pallas kernels: none -> 44 us  [fused(): pl.pallas_call(functools.partial(kernel, chips, rows_dev * n_samp, feat_c...]
    all_gather x2 -> x0, blocking collectives: 38.5 us -> none  [per_device(): lax.all_gather(packed, 'feat', axis=0, tiled=True)]
    reduce_scatter x2 -> x0, waiting for transfers between devices: 26.4 us -> none  [per_device(): lax.psum_scatter(lax.dot_general(regrouped, weighted, (((0,), (0,)), ((),...]
    all_to_all x1 -> x0, starting transfers between devices: 4.38 us -> none  [per_device(): lax.all_to_all(grads, 'feat', split_axis=0, concat_axis=1, tiled=True)]
    dot_general x4 -> x0, matrix products: 4.03 us -> none  [the longest x2 3.1 us: per_device(): lax.dot_general(regrouped, weighted, (((0,), (0,)), ((), ())), preferred_...]
    unnamed x8 -> x3, local copies, waits for them, and re-layouts: 1.36 us -> 5.22 us
    all_to_all x1 -> x0, local copies, waits for them, and re-layouts: 2.91 us -> none  [per_device(): lax.all_to_all(grads, 'feat', split_axis=0, concat_axis=1, tiled=True)]
  transfers between devices with their start and end apart: 3 -> 0, of which waited for: 2 -> 0; matrix products, arithmetic and copies ran while one was open for 0% -> 0% of each run, Pallas kernels for 0% -> 0%
where the time goes in v1:
time: 50.2 us; the launch traced here: 49.9 us
  Pallas kernels  44 us (88%)
  local copies, waits for them, and re-layouts  5.22 us (10%)
  between operations  0.64 us (1%)
    pallas_call x1, Pallas kernels, fused(): pl.pallas_call(functools.partial(kernel, chips, rows_dev * n_samp, feat_c...  44 us
    unnamed x3, local copies, waits for them, and re-layouts  5.22 us

profile of v1, /device:TPU:0, one launch (start us, length us, event | category | flops | bytes accessed | tf_op | source)
XLA Modules:
  0.0 49.9 jit_solution(2745064057858106117)
XLA Ops:
  0.6 44.0 %cg.1 = (f32[64,256]{1,0:T(8,128)}, f32[64,2048]{1,0:T(8,128)}, f32[64,2048]{1,0:T(8,128)}) custom-call(bf16[512,2048]{1,0:T(8,128)(2,1)} %grads_ref.1, f32[1,512]{1,0:T(1,128)} %bitcast.9, f32[64,2048]{1,0:T(8,128)} %bitcast.7), custom_call_target="tpu_custom_call" | custom-call | tf_op jit(solution)/shard_map/cg/pallas_call | solution.py:207
  44.7 1.5 %copy.9 = f32[256,64]{0,1:T(8,128)} copy(f32[256,64]{0,1:T(8,128)} %bitcast.8) | data formatting | bytes 131072
  46.1 1.9 %copy.10 = f32[2048,64]{0,1:T(8,128)} copy(f32[2048,64]{0,1:T(8,128)} %bitcast.6) | data formatting | bytes 1048576
  48.0 1.9 %copy.11 = f32[2048,64]{0,1:T(8,128)} copy(f32[2048,64]{0,1:T(8,128)} %bitcast.5) | data formatting | bytes 1048576

commit v2 on v1

--- a/solution.py
+++ b/solution.py
@@ -10,6 +10,7 @@
 
 ITERS = 2
 LANES = 128
+VMEM_BYTES = 16 * 2**20
 MESH = pl.DeviceIdType.MESH
 
 damping_term = 0.1
@@ -45,8 +46,10 @@
     chip = lax.div(samp, 2)
     dirs, width = targets_ref.shape
     rows_dev = grads_ref.shape[0]
+    half = rows_dev // 2
     partner = (samp + 1 - 2 * core, feat)
     mirror = (samp, 1 - feat)
+    wide_half = chips * LANES
 
     def peer(offset):
         other = lax.rem(chip + offset, chips)
@@ -61,92 +64,129 @@
             src_ref=src, dst_ref=dst, send_sem=send, recv_sem=recv, device_id=device, device_id_type=MESH
         )
 
-    scaled = weights_ref[...] / total
+    def lanes_of(which):
+        return pl.ds(pl.multiple_of(which * wide_half, wide_half), wide_half)
+
+    own_half, other_half = lanes_of(core), lanes_of(1 - core)
     own_lanes = pl.ds(pl.multiple_of((core * chips + chip) * LANES, LANES), LANES)
-    target_slice = targets_ref[:, own_lanes]
+    nt = (((1,), (1,)), ((), ()))
+
+    def joined(step, which):
+        return jnp.concatenate([gathered[step, which, i] for i in range(chips)], axis=1)
 
     for step in range(ITERS):
-        targets = targets_ref[...]
-        if step == 0:
+        mine = []
+        copies = []
+        if step == 0:
+            targets = targets_ref[...]
             packed = targets.astype(jnp.bfloat16)
+        else:
+            near = joined(step - 1, core)
+            started = [
+                lax.dot_general(
+                    near, grads_ref[h * half : (h + 1) * half, own_half], nt,
+                    preferred_element_type=jnp.float32)
+                for h in range(2)
+            ]
+            for i in range(chips):
+                remote(
+                    gathered.at[step - 1, 1 - core, i], gathered.at[step - 1, 1 - core, i],
+                    pair_send.at[step - 1, 2 + i], pair_recv.at[step - 1, 2 + i], partner).wait_recv()
+            far = joined(step - 1, 1 - core)
+        for h in range(2):
+            rows_h = slice(h * half, (h + 1) * half)
+            if step == 0:
+                part = lax.dot_general(
+                    packed, grads_ref[rows_h, :], nt, preferred_element_type=jnp.float32)
+            else:
+                part = started[h] + lax.dot_general(
+                    far, grads_ref[rows_h, other_half], nt, preferred_element_type=jnp.float32)
+            rows_out[step, h] = part.astype(jnp.bfloat16)
+            if step == 0 and h == 0:
+                pl.semaphore_wait(barrier, chips + 1)
+            copies.append(remote(
+                rows_out.at[step, h], rows_in.at[step, h],
+                feat_send.at[step, h], feat_recv.at[step, h], mirror))
+            copies[-1].start()
+            mine.append(part)
+        if step == 0:
             sums = [jnp.sum(targets * targets, axis=1, keepdims=True)]
         else:
-            packed = jnp.concatenate(
-                [gathered[step - 1, c, i] for c in range(2) for i in range(chips)], axis=1
-            )
-            wide = packed.astype(jnp.float32)
-            sums = [
-                jnp.sum(wide * wide, axis=1, keepdims=True),
-                jnp.sum(wide * targets, axis=1, keepdims=True),
-            ]
-        own = lax.dot_general(
-            packed, grads_ref[...], (((1,), (1,)), ((), ())), preferred_element_type=jnp.float32
-        )
-        rows_out[step] = own.astype(jnp.bfloat16)
+            pieces = [(near, own_half), (far, other_half)]
+            sums = [0.0, 0.0]
+            for block, lanes in pieces:
+                block = block.astype(jnp.float32)
+                sums[0] = sums[0] + jnp.sum(block * block, axis=1, keepdims=True)
+                sums[1] = sums[1] + jnp.sum(block * targets_ref[:, lanes], axis=1, keepdims=True)
         tile_out[step] = pack_columns(sums)
-        if step == 0:
-            pl.semaphore_wait(barrier, chips + 1)
-        copies = [
-            remote(rows_out.at[step], rows_in.at[step], feat_send.at[step, 0], feat_recv.at[step, 0], mirror),
-            remote(tile_out.at[step], tile_in.at[step], feat_send.at[step, 1], feat_recv.at[step, 1], mirror),
-        ]
-        for copy in copies:
-            copy.start()
-        for copy in copies:
-            copy.wait()
-        rows = own + rows_in[step].astype(jnp.float32)
-        sums = unpack_columns(tile_out[step] + tile_in[step], len(sums), dirs)
-        if step == 0:
-            norm = square = sums[0]
-            resid_slice = target_slice
-            direction_slice = target_slice
-            first_rows = rows
-            first_norm = norm
-        else:
+        copies.append(remote(tile_out.at[step], tile_in.at[step], feat_send.at[step, 2], feat_recv.at[step, 2], mirror))
+        copies[-1].start()
+        if step == 0:
+            scaled = weights_ref[...] / total
+            target_slice = targets_ref[:, own_lanes]
+
+        def finish_sums():
+            copies[2].wait()
+            return unpack_columns(tile_out[step] + tile_in[step], len(sums), dirs)
+
+        if step == 1:
+            sums = finish_sums()
             norm = sums[0]
             ratio = norm / first_norm
             square = norm + 2.0 * ratio * sums[1] + ratio * ratio * first_norm
-            rows = rows + ratio * first_rows
             direction_slice = resid_slice + ratio * target_slice
-        weighted = (rows * scaled).astype(jnp.bfloat16)
-        curve = jnp.sum(weighted.astype(jnp.float32) * rows, axis=1, keepdims=True)
-        image = jnp.dot(weighted, grads_ref[...], preferred_element_type=jnp.float32)
-        for c in range(2):
-            for i in range(chips):
-                at = (c * chips + i) * LANES
-                block = image[:, at : at + LANES]
-                image_f32[c, i] = block
-                image_b16[step, c, i] = block.astype(jnp.bfloat16)
-        pair_tile_out[step] = pack_columns([curve])
-        copies = [
-            remote(image_b16.at[step, 1 - core], pair_in.at[step], pair_send.at[step, 0], pair_recv.at[step, 0], partner),
-            remote(pair_tile_out.at[step], pair_tile_in.at[step], pair_send.at[step, 1], pair_recv.at[step, 1], partner),
-        ]
-        for copy in copies:
-            copy.start()
-        for copy in copies:
-            copy.wait()
-        image_f32[core] = image_f32[core] + pair_in[step].astype(jnp.float32)
-        chip_out[step] = image_f32[core].astype(jnp.bfloat16)
+        rows, curve = [], 0.0
+        toward = mine_image = None
+        for h in range(2):
+            rows_h = slice(h * half, (h + 1) * half)
+            copies[h].wait()
+            whole = mine[h] + rows_in[step, h].astype(jnp.float32)
+            if step == 1:
+                whole = whole + ratio * first_rows[h]
+            rows.append(whole)
+            weighted = (whole * scaled[:, rows_h]).astype(jnp.bfloat16)
+            there = jnp.dot(weighted, grads_ref[rows_h, other_half], preferred_element_type=jnp.float32)
+            toward = there if h == 0 else toward + there
+            if h == 1:
+                for i in range(chips):
+                    image_b16[step, i] = toward[:, i * LANES : (i + 1) * LANES].astype(jnp.bfloat16)
+                swap = remote(image_b16.at[step], pair_in.at[step], pair_send.at[step, 0], pair_recv.at[step, 0], partner)
+                swap.start()
+            curve = curve + jnp.sum(weighted.astype(jnp.float32) * whole, axis=1, keepdims=True)
+            if h == 1:
+                pair_tile_out[step] = pack_columns([curve])
+                swap_tile = remote(
+                    pair_tile_out.at[step], pair_tile_in.at[step], pair_send.at[step, 1], pair_recv.at[step, 1], partner)
+                swap_tile.start()
+            here = jnp.dot(weighted, grads_ref[rows_h, own_half], preferred_element_type=jnp.float32)
+            mine_image = here if h == 0 else mine_image + here
+        if step == 0:
+            first_rows = rows
+            sums = finish_sums()
+            first_norm = norm = square = sums[0]
+            resid_slice = direction_slice = target_slice
+        swap_tile.wait()
         chip_tiles[step, chip] = pair_tile_out[step] + pair_tile_in[step]
         sends = []
+        for d in range(1, chips):
+            other, device = peer(d)
+            sends.append(remote(
+                chip_tiles.at[step, chip], chip_tiles.at[step, chip],
+                chip_send.at[step, 1, d], chip_recv.at[step, 1, chip], device))
+            sends[-1].start()
+        swap.wait()
+        for i in range(chips):
+            both = mine_image[:, i * LANES : (i + 1) * LANES] + pair_in[step, i].astype(jnp.float32)
+            image_f32[i] = both
+            chip_out[step, i] = both.astype(jnp.bfloat16)
         for d in range(1, chips):
             other, device = peer(d)
             sends.append(remote(
                 chip_out.at[step, other], chip_in.at[step, chip],
                 chip_send.at[step, 0, d], chip_recv.at[step, 0, chip], device))
-            sends.append(remote(
-                chip_tiles.at[step, chip], chip_tiles.at[step, chip],
-                chip_send.at[step, 1, d], chip_recv.at[step, 1, chip], device))
-        for copy in sends:
-            copy.start()
-        reduced = image_f32[core, chip]
-        for d in range(1, chips):
-            other, device = peer(d)
-            remote(
-                chip_out.at[step, other], chip_in.at[step, other],
-                chip_send.at[step, 0, d], chip_recv.at[step, 0, other], device).wait_recv()
-            reduced = reduced + chip_in[step, other].astype(jnp.float32)
+            sends[-1].start()
+        for d in range(1, chips):
+            other, device = peer(d)
             remote(
                 chip_tiles.at[step, other], chip_tiles.at[step, other],
                 chip_send.at[step, 1, d], chip_recv.at[step, 1, other], device).wait_recv()
@@ -155,7 +195,14 @@
             curve_tile = curve_tile + chip_tiles[step, i]
         curvature = unpack_columns(curve_tile, 1, dirs)[0] + damping_term * square
         alpha = norm / curvature
-        resid_slice = resid_slice - alpha * (reduced + damping_term * direction_slice)
+        reduced = image_f32[chip] + damping_term * direction_slice
+        for d in range(1, chips):
+            other, device = peer(d)
+            remote(
+                chip_out.at[step, other], chip_in.at[step, other],
+                chip_send.at[step, 0, d], chip_recv.at[step, 0, other], device).wait_recv()
+            reduced = reduced + chip_in[step, other].astype(jnp.float32)
+        resid_slice = resid_slice - alpha * reduced
         gathered[step, core, chip] = resid_slice.astype(jnp.bfloat16)
         spread = []
         for d in range(1, chips):
@@ -163,15 +210,25 @@
             spread.append(remote(
                 gathered.at[step, core, chip], gathered.at[step, core, chip],
                 chip_send.at[step, 2, d], chip_recv.at[step, 2, chip], device))
-        for copy in spread:
-            copy.start()
+            spread[-1].start()
+
+        def forward(which):
+            spread.append(remote(
+                gathered.at[step, core, which], gathered.at[step, core, which],
+                pair_send.at[step, 2 + which], pair_recv.at[step, 2 + which], partner))
+            spread[-1].start()
+
+        forward(chip)
         if step == 0:
             first_alpha = alpha
         else:
-            scores = (first_alpha * first_rows + alpha * rows) / math.sqrt(full_width)
-            share = rows_dev // 2
-            scores_ref[...] = jnp.where(feat == 0, scores[:, :share], scores[:, share:])
-            solution_ref[...] = first_alpha * targets + alpha * (wide + ratio * targets)
+            scores = [
+                (first_alpha * first_rows[h] + alpha * rows[h]) / math.sqrt(full_width) for h in range(2)
+            ]
+            scores_ref[...] = jnp.where(feat == 0, scores[0], scores[1])
+            for block, lanes in pieces:
+                start = targets_ref[:, lanes]
+                solution_ref[:, lanes] = first_alpha * start + alpha * (block.astype(jnp.float32) + ratio * start)
         for copy in sends:
             copy.wait_send()
         for d in range(1, chips):
@@ -179,20 +236,16 @@
             remote(
                 gathered.at[step, core, other], gathered.at[step, core, other],
                 chip_send.at[step, 2, d], chip_recv.at[step, 2, other], device).wait_recv()
-        swap = remote(
-            gathered.at[step, core], gathered.at[step, core],
-            pair_send.at[step, 2], pair_recv.at[step, 2], partner)
-        swap.start()
+            forward(other)
+        if step == ITERS - 1:
+            resid_ref[:, own_half] = joined(step, core).astype(jnp.float32)
+            for i in range(chips):
+                remote(
+                    gathered.at[step, 1 - core, i], gathered.at[step, 1 - core, i],
+                    pair_send.at[step, 2 + i], pair_recv.at[step, 2 + i], partner).wait_recv()
+            resid_ref[:, other_half] = joined(step, 1 - core).astype(jnp.float32)
         for copy in spread:
             copy.wait_send()
-        swap.wait_send()
-        remote(
-            gathered.at[step, 1 - core], gathered.at[step, 1 - core],
-            pair_send.at[step, 2], pair_recv.at[step, 2], partner).wait_recv()
-    for c in range(2):
-        for i in range(chips):
-            at = (c * chips + i) * LANES
-            resid_ref[:, at : at + LANES] = gathered[ITERS - 1, c, i].astype(jnp.float32)
 
 
 def fused(grads, weights, targets):
@@ -214,12 +267,12 @@
         in_specs=[vmem] * 3,
         out_specs=[vmem] * 3,
         scratch_shapes=[
-            pltpu.VMEM((ITERS, dirs, rows_dev), b16),
-            pltpu.VMEM((ITERS, dirs, rows_dev), b16),
+            pltpu.VMEM((ITERS, 2, dirs, rows_dev // 2), b16),
+            pltpu.VMEM((ITERS, 2, dirs, rows_dev // 2), b16),
             pltpu.VMEM((ITERS, 8, LANES), f32),
             pltpu.VMEM((ITERS, 8, LANES), f32),
-            pltpu.VMEM((2, chips, dirs, LANES), f32),
-            pltpu.VMEM((ITERS, 2, chips, dirs, LANES), b16),
+            pltpu.VMEM((chips, dirs, LANES), f32),
+            pltpu.VMEM((ITERS, chips, dirs, LANES), b16),
             pltpu.VMEM((ITERS, chips, dirs, LANES), b16),
             pltpu.VMEM((ITERS, 8, LANES), f32),
             pltpu.VMEM((ITERS, 8, LANES), f32),
@@ -227,11 +280,11 @@
             pltpu.VMEM((ITERS, chips, dirs, LANES), b16),
             pltpu.VMEM((ITERS, chips, 8, LANES), f32),
             pltpu.VMEM((ITERS, 2, chips, dirs, LANES), b16),
-            dma((ITERS, 2)), dma((ITERS, 2)),
             dma((ITERS, 3)), dma((ITERS, 3)),
+            dma((ITERS, 2 + chips)), dma((ITERS, 2 + chips)),
             dma((ITERS, 3, chips)), dma((ITERS, 3, chips)),
         ],
-        compiler_params=pltpu.CompilerParams(collective_id=0, has_side_effects=True),
+        compiler_params=pltpu.CompilerParams(collective_id=0, has_side_effects=True, vmem_limit_bytes=VMEM_BYTES),
         name="cg",
     )(grads, weights[None, :], targets.T)
     return scores.T, solved.T, resid.T

time: 50.2 us -> 47.6 us (0.948)
  Pallas kernels: 44 us -> 41.3 us
    pallas_call x1, Pallas kernels: 44 us -> 41.3 us  [fused(): pl.pallas_call(functools.partial(kernel, chips, rows_dev * n_samp, feat_c...]
    unnamed x3 -> x9, local copies, waits for them, and re-layouts: 5.22 us -> 5.52 us
where the time goes in v2:
time: 47.6 us; the launch traced here: 47.4 us
  Pallas kernels  41.3 us (87%)
  local copies, waits for them, and re-layouts  5.52 us (12%)
  between operations  0.65 us (1%)
    pallas_call x1, Pallas kernels, fused(): pl.pallas_call(functools.partial(kernel, chips, rows_dev * n_samp, feat_c...  41.3 us
    unnamed x9, local copies, waits for them, and re-layouts  5.52 us

profile of v2, /device:TPU:0, one launch (start us, length us, event | category | flops | bytes accessed | tf_op | source)
XLA Modules:
  0.0 47.4 jit_solution(3147331600805895018)
XLA Ops:
  0.6 0.0 copy-start
  0.6 1.6 %copy-done = bf16[512,2048]{1,0:T(8,128)(2,1)S(1)} copy-done((bf16[512,2048]{1,0:T(8,128)(2,1)S(1)}, bf16[512,2048]{1,0:T(8,128)(2,1)}, u32[]{:S(2)}) %copy-start) | copy-done | bytes 2097176
  2.2 0.0 copy-start.1
  2.2 1.0 %copy-done.1 = f32[2048,64]{0,1:T(8,128)S(1)} copy-done((f32[2048,64]{0,1:T(8,128)S(1)}, f32[2048,64]{0,1:T(8,128)}, u32[]{:S(2)}) %copy-start.1) | copy-done | bytes 524312
  3.3 0.0 copy-start.2
  3.3 0.7 %copy-done.2 = f32[512]{0:T(512)S(1)} copy-done((f32[512]{0:T(512)S(1)}, f32[512]{0:T(512)}, u32[]{:S(2)}) %copy-start.2) | copy-done | bytes 2072
  3.9 41.3 %cg.1 = (f32[64,256]{1,0:T(8,128)S(1)}, f32[64,2048]{1,0:T(8,128)S(1)}, f32[64,2048]{1,0:T(8,128)S(1)}) custom-call(bf16[512,2048]{1,0:T(8,128)(2,1)S(1)} %copy-done, f32[1,512]{1,0:T(1,128)S(1)} %bitcast.9, f32[64,2048]{1,0:T(8,128)S(1)} %bitcast.7), custom_call_target="tpu_custom_call" | custom-call | tf_op jit(solution)/shard_map/cg/pallas_call | solution.py:260
  45.2 0.6 %copy.9 = f32[256,64]{0,1:T(8,128)} copy(f32[256,64]{0,1:T(8,128)S(1)} %bitcast.8) | data formatting | bytes 131072
  45.8 0.8 %copy.10 = f32[2048,64]{0,1:T(8,128)} copy(f32[2048,64]{0,1:T(8,128)S(1)} %bitcast.6) | data formatting | bytes 1048576
  46.6 0.8 %copy.11 = f32[2048,64]{0,1:T(8,128)} copy(f32[2048,64]{0,1:T(8,128)S(1)} %bitcast.5) | data formatting | bytes 1048576
Async XLA Ops:
  0.6 1.6 %copy-start = (bf16[512,2048]{1,0:T(8,128)(2,1)S(1)}, bf16[512,2048]{1,0:T(8,128)(2,1)}, u32[]{:S(2)}) copy-start(bf16[512,2048]{1,0:T(8,128)(2,1)} %grads_ref.1) | copy-start | bytes 6291460
  2.2 1.0 %copy-start.1 = (f32[2048,64]{0,1:T(8,128)S(1)}, f32[2048,64]{0,1:T(8,128)}, u32[]{:S(2)}) copy-start(f32[2048,64]{0,1:T(8,128)} %param.5) | copy-start | bytes 1572868
  3.3 0.7 %copy-start.2 = (f32[512]{0:T(512)S(1)}, f32[512]{0:T(512)}, u32[]{:S(2)}) copy-start(f32[512]{0:T(512)} %param.4) | copy-start | bytes 6148

commit v3 on v0

--- a/solution.py
+++ b/solution.py
@@ -1,14 +1,308 @@
+import functools
 import math
 
 import jax
 import jax.numpy as jnp
 from jax import lax
+from jax.experimental import pallas as pl
+from jax.experimental.pallas import tpu as pltpu
 from jax.sharding import PartitionSpec as P
 
 ITERS = 2
-
+LANES = 128
+BATCHES = 2
+VMEM_BYTES = 16 * 2**20
+MESH = pl.DeviceIdType.MESH
 
 damping_term = 0.1
+
+
+def pack_columns(columns):
+    dirs = columns[0].shape[0]
+    lane = lax.broadcasted_iota(jnp.int32, (dirs, LANES), 1)
+    tile = jnp.zeros((dirs, LANES), jnp.float32)
+    for position, column in enumerate(columns):
+        tile = jnp.where(lane == position, column, tile)
+    if dirs < LANES:
+        tile = jnp.concatenate([tile, jnp.zeros((LANES - dirs, LANES), jnp.float32)], axis=0)
+    return tile.T[:8]
+
+
+def unpack_columns(tile, count, dirs):
+    padded = jnp.concatenate([tile, jnp.zeros((LANES - 8, LANES), jnp.float32)], axis=0).T
+    return [padded[:dirs, i : i + 1] for i in range(count)]
+
+
+def kernel(
+    chips, total, full_width,
+    grads_ref, weights_ref, targets_ref,
+    scores_ref, solution_ref, resid_ref,
+    rows_out, rows_in, tile_out, tile_in,
+    image_f32, image_b16, pair_in, pair_tile_out, pair_tile_in,
+    chip_out, chip_in, chip_tiles, gathered,
+    feat_send, feat_recv, pair_send, pair_recv, chip_send, chip_recv,
+):
+    samp, feat = lax.axis_index("samp"), lax.axis_index("feat")
+    core = lax.rem(samp, 2)
+    chip = lax.div(samp, 2)
+    dirs = targets_ref.shape[0] // BATCHES
+    rows_dev = grads_ref.shape[0]
+    half = rows_dev // 2
+    partner = (samp + 1 - 2 * core, feat)
+    mirror = (samp, 1 - feat)
+    wide_half = chips * LANES
+
+    def peer(offset):
+        other = lax.rem(chip + offset, chips)
+        return other, (other * 2 + core, feat)
+
+    barrier = pltpu.get_barrier_semaphore()
+    for device in [partner, mirror] + [peer(d)[1] for d in range(1, chips)]:
+        pl.semaphore_signal(barrier, inc=1, device_id=device, device_id_type=MESH)
+
+    def remote(src, dst, send, recv, device):
+        return pltpu.make_async_remote_copy(
+            src_ref=src, dst_ref=dst, send_sem=send, recv_sem=recv, device_id=device, device_id_type=MESH
+        )
+
+    def lanes_of(which):
+        return pl.ds(pl.multiple_of(which * wide_half, wide_half), wide_half)
+
+    own_half, other_half = lanes_of(core), lanes_of(1 - core)
+    own_lanes = pl.ds(pl.multiple_of((core * chips + chip) * LANES, LANES), LANES)
+    nt = (((1,), (1,)), ((), ()))
+
+    def joined(step, which):
+        return jnp.concatenate([gathered[step, which, i] for i in range(chips)], axis=1)
+
+    def solve(batch):
+        lines = slice(batch * dirs, (batch + 1) * dirs)
+        for step in range(ITERS):
+            at = step * BATCHES + batch
+            mine = []
+            copies = []
+            if step == 0:
+                targets = targets_ref[lines, :]
+                packed = targets.astype(jnp.bfloat16)
+            else:
+                near = joined(at - BATCHES, core)
+                started = [
+                    lax.dot_general(
+                        near, grads_ref[h * half : (h + 1) * half, own_half], nt,
+                        preferred_element_type=jnp.float32)
+                    for h in range(2)
+                ]
+                yield
+                for i in range(chips):
+                    remote(
+                        gathered.at[at - BATCHES, 1 - core, i], gathered.at[at - BATCHES, 1 - core, i],
+                        pair_send.at[at - BATCHES, 2 + i], pair_recv.at[at - BATCHES, 2 + i], partner).wait_recv()
+                far = joined(at - BATCHES, 1 - core)
+            for h in range(2):
+                rows_h = slice(h * half, (h + 1) * half)
+                if step == 0:
+                    part = lax.dot_general(
+                        packed, grads_ref[rows_h, :], nt, preferred_element_type=jnp.float32)
+                else:
+                    part = started[h] + lax.dot_general(
+                        far, grads_ref[rows_h, other_half], nt, preferred_element_type=jnp.float32)
+                rows_out[at, h] = part.astype(jnp.bfloat16)
+                if step == 0 and h == 0 and batch == 0:
+                    pl.semaphore_wait(barrier, chips + 1)
+                copies.append(remote(
+                    rows_out.at[at, h], rows_in.at[at, h],
+                    feat_send.at[at, h], feat_recv.at[at, h], mirror))
+                copies[-1].start()
+                mine.append(part)
+            if step == 0:
+                sums = [jnp.sum(targets * targets, axis=1, keepdims=True)]
+            else:
+                pieces = [(near, own_half), (far, other_half)]
+                sums = [0.0, 0.0]
+                for block, lanes in pieces:
+                    block = block.astype(jnp.float32)
+                    sums[0] = sums[0] + jnp.sum(block * block, axis=1, keepdims=True)
+                    sums[1] = sums[1] + jnp.sum(block * targets_ref[lines, lanes], axis=1, keepdims=True)
+            tile_out[at] = pack_columns(sums)
+            copies.append(remote(tile_out.at[at], tile_in.at[at], feat_send.at[at, 2], feat_recv.at[at, 2], mirror))
+            copies[-1].start()
+            if step == 0:
+                scaled = weights_ref[...] / total
+                target_slice = targets_ref[lines, own_lanes]
+
+            def finish_sums():
+                copies[2].wait()
+                return unpack_columns(tile_out[at] + tile_in[at], len(sums), dirs)
+
+            yield
+            if step == 1:
+                sums = finish_sums()
+                norm = sums[0]
+                ratio = norm / first_norm
+                square = norm + 2.0 * ratio * sums[1] + ratio * ratio * first_norm
+                direction_slice = resid_slice + ratio * target_slice
+            rows, curve = [], 0.0
+            toward = mine_image = None
+            for h in range(2):
+                rows_h = slice(h * half, (h + 1) * half)
+                copies[h].wait()
+                whole = mine[h] + rows_in[at, h].astype(jnp.float32)
+                if step == 1:
+                    whole = whole + ratio * first_rows[h]
+                rows.append(whole)
+                weighted = (whole * scaled[:, rows_h]).astype(jnp.bfloat16)
+                there = jnp.dot(weighted, grads_ref[rows_h, other_half], preferred_element_type=jnp.float32)
+                toward = there if h == 0 else toward + there
+                if h == 1:
+                    for i in range(chips):
+                        image_b16[at, i] = toward[:, i * LANES : (i + 1) * LANES].astype(jnp.bfloat16)
+                    swap = remote(image_b16.at[at], pair_in.at[at], pair_send.at[at, 0], pair_recv.at[at, 0], partner)
+                    swap.start()
+                curve = curve + jnp.sum(weighted.astype(jnp.float32) * whole, axis=1, keepdims=True)
+                if h == 1:
+                    pair_tile_out[at] = pack_columns([curve])
+                    swap_tile = remote(
+                        pair_tile_out.at[at], pair_tile_in.at[at], pair_send.at[at, 1], pair_recv.at[at, 1], partner)
+                    swap_tile.start()
+                here = jnp.dot(weighted, grads_ref[rows_h, own_half], preferred_element_type=jnp.float32)
+                mine_image = here if h == 0 else mine_image + here
+            if step == 0:
+                first_rows = rows
+                sums = finish_sums()
+                first_norm = norm = square = sums[0]
+                resid_slice = direction_slice = target_slice
+            yield
+            swap_tile.wait()
+            chip_tiles[at, chip] = pair_tile_out[at] + pair_tile_in[at]
+            sends = []
+            for d in range(1, chips):
+                other, device = peer(d)
+                sends.append(remote(
+                    chip_tiles.at[at, chip], chip_tiles.at[at, chip],
+                    chip_send.at[at, 1, d], chip_recv.at[at, 1, chip], device))
+                sends[-1].start()
+            swap.wait()
+            for i in range(chips):
+                both = mine_image[:, i * LANES : (i + 1) * LANES] + pair_in[at, i].astype(jnp.float32)
+                image_f32[batch, i] = both
+                chip_out[at, i] = both.astype(jnp.bfloat16)
+            for d in range(1, chips):
+                other, device = peer(d)
+                sends.append(remote(
+                    chip_out.at[at, other], chip_in.at[at, chip],
+                    chip_send.at[at, 0, d], chip_recv.at[at, 0, chip], device))
+                sends[-1].start()
+            yield
+            for d in range(1, chips):
+                other, device = peer(d)
+                remote(
+                    chip_tiles.at[at, other], chip_tiles.at[at, other],
+                    chip_send.at[at, 1, d], chip_recv.at[at, 1, other], device).wait_recv()
+            curve_tile = chip_tiles[at, 0]
+            for i in range(1, chips):
+                curve_tile = curve_tile + chip_tiles[at, i]
+            curvature = unpack_columns(curve_tile, 1, dirs)[0] + damping_term * square
+            alpha = norm / curvature
+            reduced = image_f32[batch, chip] + damping_term * direction_slice
+            for d in range(1, chips):
+                other, device = peer(d)
+                remote(
+                    chip_out.at[at, other], chip_in.at[at, other],
+                    chip_send.at[at, 0, d], chip_recv.at[at, 0, other], device).wait_recv()
+                reduced = reduced + chip_in[at, other].astype(jnp.float32)
+            resid_slice = resid_slice - alpha * reduced
+            gathered[at, core, chip] = resid_slice.astype(jnp.bfloat16)
+            spread = []
+            for d in range(1, chips):
+                other, device = peer(d)
+                spread.append(remote(
+                    gathered.at[at, core, chip], gathered.at[at, core, chip],
+                    chip_send.at[at, 2, d], chip_recv.at[at, 2, chip], device))
+                spread[-1].start()
+
+            def forward(which):
+                spread.append(remote(
+                    gathered.at[at, core, which], gathered.at[at, core, which],
+                    pair_send.at[at, 2 + which], pair_recv.at[at, 2 + which], partner))
+                spread[-1].start()
+
+            forward(chip)
+            if step == 0:
+                first_alpha = alpha
+            else:
+                scores = [
+                    (first_alpha * first_rows[h] + alpha * rows[h]) / math.sqrt(full_width) for h in range(2)
+                ]
+                scores_ref[lines, :] = jnp.where(feat == 0, scores[0], scores[1])
+                for block, lanes in pieces:
+                    start = targets_ref[lines, lanes]
+                    solution_ref[lines, lanes] = first_alpha * start + alpha * (block.astype(jnp.float32) + ratio * start)
+            yield
+            for copy in sends:
+                copy.wait_send()
+            for d in range(1, chips):
+                other, device = peer(d)
+                remote(
+                    gathered.at[at, core, other], gathered.at[at, core, other],
+                    chip_send.at[at, 2, d], chip_recv.at[at, 2, other], device).wait_recv()
+                forward(other)
+            if step == ITERS - 1:
+                resid_ref[lines, own_half] = joined(at, core).astype(jnp.float32)
+                yield
+                for i in range(chips):
+                    remote(
+                        gathered.at[at, 1 - core, i], gathered.at[at, 1 - core, i],
+                        pair_send.at[at, 2 + i], pair_recv.at[at, 2 + i], partner).wait_recv()
+                resid_ref[lines, other_half] = joined(at, 1 - core).astype(jnp.float32)
+            for copy in spread:
+                copy.wait_send()
+
+    running = [solve(batch) for batch in range(BATCHES)]
+    while running:
+        running = [one for one in running if next(one, True) is None]
+
+
+def fused(grads, weights, targets):
+    rows_dev, feat_cols = grads.shape
+    n_samp = lax.axis_size("samp")
+    n_feat = lax.axis_size("feat")
+    dirs = targets.shape[1]
+    slots, lines = ITERS * BATCHES, dirs // BATCHES
+    chips = n_samp // 2
+    f32, b16 = jnp.float32, jnp.bfloat16
+    vmem = pl.BlockSpec(memory_space=pltpu.VMEM)
+    dma = pltpu.SemaphoreType.DMA
+    scores, solved, resid = pl.pallas_call(
+        functools.partial(kernel, chips, rows_dev * n_samp, feat_cols * n_feat),
+        out_shape=(
+            jax.ShapeDtypeStruct((dirs, rows_dev // n_feat), f32),
+            jax.ShapeDtypeStruct((dirs, feat_cols), f32),
+            jax.ShapeDtypeStruct((dirs, feat_cols), f32),
+        ),
+        in_specs=[vmem] * 3,
+        out_specs=[vmem] * 3,
+        scratch_shapes=[
+            pltpu.VMEM((slots, 2, lines, rows_dev // 2), b16),
+            pltpu.VMEM((slots, 2, lines, rows_dev // 2), b16),
+            pltpu.VMEM((slots, 8, LANES), f32),
+            pltpu.VMEM((slots, 8, LANES), f32),
+            pltpu.VMEM((BATCHES, chips, lines, LANES), f32),
+            pltpu.VMEM((slots, chips, lines, LANES), b16),
+            pltpu.VMEM((slots, chips, lines, LANES), b16),
+            pltpu.VMEM((slots, 8, LANES), f32),
+            pltpu.VMEM((slots, 8, LANES), f32),
+            pltpu.VMEM((slots, chips, lines, LANES), b16),
+            pltpu.VMEM((slots, chips, lines, LANES), b16),
+            pltpu.VMEM((slots, chips, 8, LANES), f32),
+            pltpu.VMEM((slots, 2, chips, lines, LANES), b16),
+            dma((slots, 3)), dma((slots, 3)),
+            dma((slots, 2 + chips)), dma((slots, 2 + chips)),
+            dma((slots, 3, chips)), dma((slots, 3, chips)),
+        ],
+        compiler_params=pltpu.CompilerParams(collective_id=0, has_side_effects=True, vmem_limit_bytes=VMEM_BYTES),
+        name="cg",
+    )(grads, weights[None, :], targets.T)
+    return scores.T, solved.T, resid.T
 
 
 def per_device(grads, weights, targets):
@@ -68,9 +362,24 @@
     return (scores, solution, resid)
 
 
+def dispatch(grads, weights, targets):
+    rows_dev, feat_cols = grads.shape
+    n_samp, n_feat = lax.axis_size("samp"), lax.axis_size("feat")
+    fits = (
+        n_feat == 2
+        and n_samp % 2 == 0
+        and n_samp >= 4
+        and feat_cols == n_samp * LANES
+        and rows_dev % (2 * LANES) == 0
+        and targets.shape[1] % (16 * BATCHES) == 0
+        and targets.shape[1] <= LANES
+    )
+    return (fused if fits else per_device)(grads, weights, targets)
+
+
 def solution(mesh):
     return jax.shard_map(
-        per_device,
+        dispatch,
         mesh=mesh,
         in_specs=(P("samp", "feat"), P("samp"), P("feat", None)),
         out_specs=(P(("samp", "feat"), None), P("feat", None), P("feat", None)),

time: 244 us -> 51.5 us (0.21)
  blocking collectives: 187 us -> 0 us
  Pallas kernels: 0 us -> 45.1 us
  waiting for transfers between devices: 26.5 us -> 0 us
  between operations: 14.1 us -> 0.65 us
  starting transfers between devices: 4.42 us -> 0 us
  matrix products: 4.03 us -> 0 us
  other arithmetic: 3.03 us -> 0 us
    psum x5 -> x0, blocking collectives: 148 us -> none  [the longest x2 134 us: per_device(): image = lax.psum(partial_image, 'samp') + damping_term * direction]
    pallas_call x0 -> x1, Pallas kernels: none -> 45.1 us  [fused(): pl.pallas_call(functools.partial(kernel, chips, rows_dev * n_samp, feat_c...]
    all_gather x2 -> x0, blocking collectives: 38.5 us -> none  [per_device(): lax.all_gather(packed, 'feat', axis=0, tiled=True)]
    reduce_scatter x2 -> x0, waiting for transfers between devices: 26.4 us -> none  [per_device(): lax.psum_scatter(lax.dot_general(regrouped, weighted, (((0,), (0,)), ((),...]
    all_to_all x1 -> x0, starting transfers between devices: 4.38 us -> none  [per_device(): lax.all_to_all(grads, 'feat', split_axis=0, concat_axis=1, tiled=True)]
    unnamed x8 -> x9, local copies, waits for them, and re-layouts: 1.36 us -> 5.52 us
    dot_general x4 -> x0, matrix products: 4.03 us -> none  [the longest x2 3.1 us: per_device(): lax.dot_general(regrouped, weighted, (((0,), (0,)), ((), ())), preferred_...]
    all_to_all x1 -> x0, local copies, waits for them, and re-layouts: 2.91 us -> none  [per_device(): lax.all_to_all(grads, 'feat', split_axis=0, concat_axis=1, tiled=True)]
  transfers between devices with their start and end apart: 3 -> 0, of which waited for: 2 -> 0; matrix products, arithmetic and copies ran while one was open for 0% -> 0% of each run, Pallas kernels for 0% -> 0%
where the time goes in v3:
time: 51.5 us; the launch traced here: 51.2 us
  Pallas kernels  45.1 us (88%)
  local copies, waits for them, and re-layouts  5.52 us (11%)
  between operations  0.65 us (1%)
    pallas_call x1, Pallas kernels, fused(): pl.pallas_call(functools.partial(kernel, chips, rows_dev * n_samp, feat_c...  45.1 us
    unnamed x9, local copies, waits for them, and re-layouts  5.52 us

profile of v3, /device:TPU:0, one launch (start us, length us, event | category | flops | bytes accessed | tf_op | source)
XLA Modules:
  0.0 51.2 jit_solution(9545946226415252884)
XLA Ops:
  0.6 0.0 copy-start
  0.6 1.6 %copy-done = bf16[512,2048]{1,0:T(8,128)(2,1)S(1)} copy-done((bf16[512,2048]{1,0:T(8,128)(2,1)S(1)}, bf16[512,2048]{1,0:T(8,128)(2,1)}, u32[]{:S(2)}) %copy-start) | copy-done | bytes 2097176
  2.2 0.0 copy-start.1
  2.2 1.0 %copy-done.1 = f32[2048,64]{0,1:T(8,128)S(1)} copy-done((f32[2048,64]{0,1:T(8,128)S(1)}, f32[2048,64]{0,1:T(8,128)}, u32[]{:S(2)}) %copy-start.1) | copy-done | bytes 524312
  3.3 0.0 copy-start.2
  3.3 0.7 %copy-done.2 = f32[512]{0:T(512)S(1)} copy-done((f32[512]{0:T(512)S(1)}, f32[512]{0:T(512)}, u32[]{:S(2)}) %copy-start.2) | copy-done | bytes 2072
  3.9 45.1 %cg.1 = (f32[64,256]{1,0:T(8,128)S(1)}, f32[64,2048]{1,0:T(8,128)S(1)}, f32[64,2048]{1,0:T(8,128)S(1)}) custom-call(bf16[512,2048]{1,0:T(8,128)(2,1)S(1)} %copy-done, f32[1,512]{1,0:T(1,128)S(1)} %bitcast.9, f32[64,2048]{1,0:T(8,128)S(1)} %bitcast.7), custom_call_target="tpu_custom_call" | custom-call | tf_op jit(solution)/shard_map/cg/pallas_call | solution.py:275
  49.0 0.6 %copy.9 = f32[256,64]{0,1:T(8,128)} copy(f32[256,64]{0,1:T(8,128)S(1)} %bitcast.8) | data formatting | bytes 131072
  49.6 0.8 %copy.10 = f32[2048,64]{0,1:T(8,128)} copy(f32[2048,64]{0,1:T(8,128)S(1)} %bitcast.6) | data formatting | bytes 1048576
  50.4 0.8 %copy.11 = f32[2048,64]{0,1:T(8,128)} copy(f32[2048,64]{0,1:T(8,128)S(1)} %bitcast.5) | data formatting | bytes 1048576
Async XLA Ops:
  0.6 1.6 %copy-start = (bf16[512,2048]{1,0:T(8,128)(2,1)S(1)}, bf16[512,2048]{1,0:T(8,128)(2,1)}, u32[]{:S(2)}) copy-start(bf16[512,2048]{1,0:T(8,128)(2,1)} %grads_ref.1) | copy-start | bytes 6291460
  2.2 1.0 %copy-start.1 = (f32[2048,64]{0,1:T(8,128)S(1)}, f32[2048,64]{0,1:T(8,128)}, u32[]{:S(2)}) copy-start(f32[2048,64]{0,1:T(8,128)} %param.5) | copy-start | bytes 1572868
  3.3 0.7 %copy-start.2 = (f32[512]{0:T(512)S(1)}, f32[512]{0:T(512)}, u32[]{:S(2)}) copy-start(f32[512]{0:T(512)} %param.4) | copy-start | bytes 6148

commit v4 on v2

--- a/solution.py
+++ b/solution.py
@@ -10,7 +10,7 @@
 
 ITERS = 2
 LANES = 128
-VMEM_BYTES = 16 * 2**20
+VMEM_BYTES = 105 * 2**19
 MESH = pl.DeviceIdType.MESH
 
 damping_term = 0.1
@@ -34,12 +34,13 @@
 
 def kernel(
     chips, total, full_width,
+    grads_hbm, weights_hbm, targets_hbm,
+    scores_ref, solution_ref, resid_ref,
     grads_ref, weights_ref, targets_ref,
-    scores_ref, solution_ref, resid_ref,
     rows_out, rows_in, tile_out, tile_in,
     image_f32, image_b16, pair_in, pair_tile_out, pair_tile_in,
     chip_out, chip_in, chip_tiles, gathered,
-    feat_send, feat_recv, pair_send, pair_recv, chip_send, chip_recv,
+    load_sem, feat_send, feat_recv, pair_send, pair_recv, chip_send, chip_recv,
 ):
     samp, feat = lax.axis_index("samp"), lax.axis_index("feat")
     core = lax.rem(samp, 2)
@@ -55,6 +56,15 @@
         other = lax.rem(chip + offset, chips)
         return other, (other * 2 + core, feat)
 
+    loads = [
+        pltpu.make_async_copy(targets_hbm, targets_ref, load_sem.at[0]),
+        pltpu.make_async_copy(grads_hbm.at[pl.ds(0, half)], grads_ref.at[pl.ds(0, half)], load_sem.at[1]),
+        pltpu.make_async_copy(grads_hbm.at[pl.ds(half, half)], grads_ref.at[pl.ds(half, half)], load_sem.at[2]),
+        pltpu.make_async_copy(weights_hbm, weights_ref, load_sem.at[3]),
+    ]
+    for load in loads:
+        load.start()
+
     barrier = pltpu.get_barrier_semaphore()
     for device in [partner, mirror] + [peer(d)[1] for d in range(1, chips)]:
         pl.semaphore_signal(barrier, inc=1, device_id=device, device_id_type=MESH)
@@ -78,6 +88,7 @@
         mine = []
         copies = []
         if step == 0:
+            loads[0].wait()
             targets = targets_ref[...]
             packed = targets.astype(jnp.bfloat16)
         else:
@@ -96,6 +107,7 @@
         for h in range(2):
             rows_h = slice(h * half, (h + 1) * half)
             if step == 0:
+                loads[1 + h].wait()
                 part = lax.dot_general(
                     packed, grads_ref[rows_h, :], nt, preferred_element_type=jnp.float32)
             else:
@@ -122,6 +134,7 @@
         copies.append(remote(tile_out.at[step], tile_in.at[step], feat_send.at[step, 2], feat_recv.at[step, 2], mirror))
         copies[-1].start()
         if step == 0:
+            loads[3].wait()
             scaled = weights_ref[...] / total
             target_slice = targets_ref[:, own_lanes]
 
@@ -264,9 +277,12 @@
             jax.ShapeDtypeStruct((dirs, feat_cols), f32),
             jax.ShapeDtypeStruct((dirs, feat_cols), f32),
         ),
-        in_specs=[vmem] * 3,
+        in_specs=[pl.BlockSpec(memory_space=pltpu.HBM)] * 3,
         out_specs=[vmem] * 3,
         scratch_shapes=[
+            pltpu.VMEM((rows_dev, feat_cols), b16),
+            pltpu.VMEM((1, rows_dev), f32),
+            pltpu.VMEM((dirs, feat_cols), f32),
             pltpu.VMEM((ITERS, 2, dirs, rows_dev // 2), b16),
             pltpu.VMEM((ITERS, 2, dirs, rows_dev // 2), b16),
             pltpu.VMEM((ITERS, 8, LANES), f32),
@@ -280,6 +296,7 @@
             pltpu.VMEM((ITERS, chips, dirs, LANES), b16),
             pltpu.VMEM((ITERS, chips, 8, LANES), f32),
             pltpu.VMEM((ITERS, 2, chips, dirs, LANES), b16),
+            dma((4,)),
             dma((ITERS, 3)), dma((ITERS, 3)),
             dma((ITERS, 2 + chips)), dma((ITERS, 2 + chips)),
             dma((ITERS, 3, chips)), dma((ITERS, 3, chips)),

time: 47.6 us -> 45 us (0.945)
  local copies, waits for them, and re-layouts: 5.52 us -> 2.89 us
    unnamed x9 -> x5, local copies, waits for them, and re-layouts: 5.52 us -> 2.89 us
where the time goes in v4:
time: 45 us; the launch traced here: 44.8 us
  Pallas kernels  41.3 us (92%)
  local copies, waits for them, and re-layouts  2.89 us (6%)
  between operations  0.65 us (1%)
    pallas_call x1, Pallas kernels, fused(): pl.pallas_call(functools.partial(kernel, chips, rows_dev * n_samp, feat_c...  41.3 us
    unnamed x5, local copies, waits for them, and re-layouts  2.89 us

profile of v4, /device:TPU:0, one launch (start us, length us, event | category | flops | bytes accessed | tf_op | source)
XLA Modules:
  0.0 44.8 jit_solution(7311338441026654630)
XLA Ops:
  0.6 0.0 copy-start
  0.6 0.7 %copy-done = f32[512]{0:T(512)S(1)} copy-done((f32[512]{0:T(512)S(1)}, f32[512]{0:T(512)}, u32[]{:S(2)}) %copy-start) | copy-done | bytes 2072
  1.3 41.3 %cg.1 = (f32[64,256]{1,0:T(8,128)S(1)}, f32[64,2048]{1,0:T(8,128)S(1)}, f32[64,2048]{1,0:T(8,128)S(1)}) custom-call(bf16[512,2048]{1,0:T(8,128)(2,1)} %grads_hbm.1, f32[1,512]{1,0:T(1,128)S(1)} %bitcast.8, f32[64,2048]{1,0:T(8,128)} %bitcast.9), custom_call_target="tpu_custom_call" | custom-call | tf_op jit(solution)/shard_map/cg/pallas_call | solution.py:273
  42.6 0.6 %copy.9 = f32[256,64]{0,1:T(8,128)} copy(f32[256,64]{0,1:T(8,128)S(1)} %bitcast.7) | data formatting | bytes 131072
  43.2 0.8 %copy.10 = f32[2048,64]{0,1:T(8,128)} copy(f32[2048,64]{0,1:T(8,128)S(1)} %bitcast.6) | data formatting | bytes 1048576
  44.0 0.8 %copy.11 = f32[2048,64]{0,1:T(8,128)} copy(f32[2048,64]{0,1:T(8,128)S(1)} %bitcast.5) | data formatting | bytes 1048576
Async XLA Ops:
  0.6 0.7 %copy-start = (f32[512]{0:T(512)S(1)}, f32[512]{0:T(512)}, u32[]{:S(2)}) copy-start(f32[512]{0:T(512)} %param.4) | copy-start | bytes 6148
